TPU v7x, 32 devices: a whole 2x2x4 slice. The times are simulated.
32 devices in a mesh: batch: 8 (over y, x, core), cols: 4 (over z).
Axes of the slice: x: 2, y: 2, z: 4, core: 2. Of those that a mesh axis runs over, the one named last changes fastest.
Arguments:
- grad_up: float32 [8, 1024, 4096], P('batch', None, 'cols'), may hold values from -0.875 to 0.875
- grad_down: float32 [8, 4096, 1024], P('batch', 'cols'), may hold values from -0.875 to 0.875
- grad_query: float32 [8, 1024, 1024], P('batch', None, 'cols'), may hold values from -0.875 to 0.875
- grad_key: float32 [8, 1024, 1024], P('batch', None, 'cols'), may hold values from -0.875 to 0.875
- grad_value: float32 [8, 1024, 1024], P('batch', None, 'cols'), may hold values from -0.875 to 0.875
- grad_mixed: float32 [8, 1024, 1024], P('batch', 'cols'), may hold values from -0.875 to 0.875
- grad_norm: float32 [8, 1024], P('batch'), may hold values from -8 to 8
- weight_up: float32 [1024, 4096], P('batch', 'cols'), may hold values from -0.1875 to 0.1875
- weight_down: float32 [4096, 1024], P('cols', 'batch'), may hold values from -0.09375 to 0.09375
- weight_query: float32 [1024, 1024], P('batch', 'cols'), may hold values from -0.1875 to 0.1875
- weight_key: float32 [1024, 1024], P('batch', 'cols'), may hold values from -0.1875 to 0.1875
- weight_value: float32 [1024, 1024], P('batch', 'cols'), may hold values from -0.1875 to 0.1875
- weight_mixed: float32 [1024, 1024], P('cols', 'batch'), may hold values from -0.1875 to 0.1875
- weight_norm: float32 [1024], P('batch'), may hold values from 0.25 to 1.75
- moment_up: float32 [1024, 4096], P('batch', 'cols'), may hold values from -1.75 to 1.75
- moment_down: float32 [4096, 1024], P('cols', 'batch'), may hold values from -1.75 to 1.75
- moment_query: float32 [1024, 1024], P('batch', 'cols'), may hold values from -1.75 to 1.75
- moment_key: float32 [1024, 1024], P('batch', 'cols'), may hold values from -1.75 to 1.75
- moment_value: float32 [1024, 1024], P('batch', 'cols'), may hold values from -1.75 to 1.75
- moment_mixed: float32 [1024, 1024], P('cols', 'batch'), may hold values from -1.75 to 1.75
- moment_norm: float32 [1024], P('batch'), may hold values from -1.75 to 1.75
Outputs:
- copy_up: bfloat16 [1024, 4096], P(None, 'cols')
- copy_down: bfloat16 [4096, 1024], P('cols')
- copy_query: bfloat16 [1024, 1024], P(None, 'cols')
- copy_key: bfloat16 [1024, 1024], P(None, 'cols')
- copy_value: bfloat16 [1024, 1024], P(None, 'cols')
- copy_mixed: bfloat16 [1024, 1024], P('cols')
- copy_norm: bfloat16 [1024], replicated
- new_up: float32 [1024, 4096], P('batch', 'cols')
- new_down: float32 [4096, 1024], P('cols', 'batch')
- new_query: float32 [1024, 1024], P('batch', 'cols')
- new_key: float32 [1024, 1024], P('batch', 'cols')
- new_value: float32 [1024, 1024], P('batch', 'cols')
- new_mixed: float32 [1024, 1024], P('cols', 'batch')
- new_norm: float32 [1024], P('batch')
- state_new_up: float32 [1024, 4096], P('batch', 'cols')
- state_new_down: float32 [4096, 1024], P('cols', 'batch')
- state_new_query: float32 [1024, 1024], P('batch', 'cols')
- state_new_key: float32 [1024, 1024], P('batch', 'cols')
- state_new_value: float32 [1024, 1024], P('batch', 'cols')
- state_new_mixed: float32 [1024, 1024], P('cols', 'batch')
- state_new_norm: float32 [1024], P('batch')
All inputs are finite; a program needn't handle non-finite values.
Results may differ from a plain program's by a relative error of at most 0.008.
Values may be sent and summed in bfloat16 or wider, within the bound.
A program may use at most 64 MiB of HBM per device.

v0:
```python
import functools

import jax
import jax.numpy as jnp
from jax import lax
from jax.experimental import pallas as pl
from jax.experimental.pallas import tpu as pltpu
from jax.sharding import PartitionSpec as P

learn_rate = 0.1
hold_rate = 0.7


def body(
    grad_up,
    grad_down,
    grad_query,
    grad_key,
    grad_value,
    grad_mixed,
    grad_norm,
    weight_up,
    weight_down,
    weight_query,
    weight_key,
    weight_value,
    weight_mixed,
    weight_norm,
    moment_up,
    moment_down,
    moment_query,
    moment_key,
    moment_value,
    moment_mixed,
    moment_norm,
):
    mean_up, mean_down, mean_query, mean_key, mean_value, mean_mixed = (
        lax.psum_scatter(
            grad_up[0].astype(jnp.bfloat16), "batch", scatter_dimension=0, tiled=True
        ).astype(jnp.float32),
        lax.psum_scatter(
            grad_down[0].astype(jnp.bfloat16), "batch", scatter_dimension=1, tiled=True
        ).astype(jnp.float32),
        lax.psum_scatter(
            grad_query[0].astype(jnp.bfloat16), "batch", scatter_dimension=0, tiled=True
        ).astype(jnp.float32),
        lax.psum_scatter(
            grad_key[0].astype(jnp.bfloat16), "batch", scatter_dimension=0, tiled=True
        ).astype(jnp.float32),
        lax.psum_scatter(
            grad_value[0].astype(jnp.bfloat16), "batch", scatter_dimension=0, tiled=True
        ).astype(jnp.float32),
        lax.psum_scatter(
            grad_mixed[0].astype(jnp.bfloat16), "batch", scatter_dimension=1, tiled=True
        ).astype(jnp.float32),
    )
    whole_norm = lax.psum(grad_norm[0], "batch")
    place = lax.axis_index("batch")
    mean_norm = lax.dynamic_slice_in_dim(
        whole_norm, place * weight_norm.shape[0], weight_norm.shape[0]
    )
    mean_rate = lax.axis_size("batch") ** (-0.5)
    mean_up = mean_up * mean_rate
    mean_down = mean_down * mean_rate
    mean_query = mean_query * mean_rate
    mean_key = mean_key * mean_rate
    mean_value = mean_value * mean_rate
    mean_mixed = mean_mixed * mean_rate
    mean_norm = mean_norm * mean_rate
    state_new_up = hold_rate * moment_up + mean_up
    new_up = weight_up - learn_rate * state_new_up
    state_new_down = hold_rate * moment_down + mean_down
    new_down = weight_down - learn_rate * state_new_down
    state_new_query = hold_rate * moment_query + mean_query
    new_query = weight_query - learn_rate * state_new_query
    state_new_key = hold_rate * moment_key + mean_key
    new_key = weight_key - learn_rate * state_new_key
    state_new_value = hold_rate * moment_value + mean_value
    new_value = weight_value - learn_rate * state_new_value
    state_new_mixed = hold_rate * moment_mixed + mean_mixed
    new_mixed = weight_mixed - learn_rate * state_new_mixed
    state_new_norm = hold_rate * moment_norm + mean_norm
    new_norm = weight_norm - learn_rate * state_new_norm
    copy_up, copy_down, copy_query, copy_key, copy_value, copy_mixed, copy_norm = (
        lax.all_gather(new_up.astype(jnp.bfloat16), "batch", axis=0, tiled=True),
        lax.all_gather(new_down.astype(jnp.bfloat16), "batch", axis=1, tiled=True),
        lax.all_gather(new_query.astype(jnp.bfloat16), "batch", axis=0, tiled=True),
        lax.all_gather(new_key.astype(jnp.bfloat16), "batch", axis=0, tiled=True),
        lax.all_gather(new_value.astype(jnp.bfloat16), "batch", axis=0, tiled=True),
        lax.all_gather(new_mixed.astype(jnp.bfloat16), "batch", axis=1, tiled=True),
        lax.all_gather(new_norm.astype(jnp.bfloat16), "batch", axis=0, tiled=True),
    )
    return (
        copy_up,
        copy_down,
        copy_query,
        copy_key,
        copy_value,
        copy_mixed,
        copy_norm,
        new_up,
        new_down,
        new_query,
        new_key,
        new_value,
        new_mixed,
        new_norm,
        state_new_up,
        state_new_down,
        state_new_query,
        state_new_key,
        state_new_value,
        state_new_mixed,
        state_new_norm,
    )


PIECES = (4, 4, 1, 1, 1, 1)
DELAYS = (0, 1, 2, 3, 4, 5, 6)
STEP_ORDER = (0, 1, 2, 3, 4, 5, 6)
X_FIRST = (0, 2, 3)
Y_FIRST = (1, 5, 4)
BY_ROWS = (True, False, True, True, True, False)
LOAD, SEND, RECV, OWN, NEW, STATE, KINDS = 0, 1, 7, 13, 14, 15, 16


def pieces_of(shapes):
    lists = []
    for names, x_first in ((X_FIRST, True), (Y_FIRST, False)):
        lists.append([])
        for m in names:
            rows = shapes[m][0] // PIECES[m]
            for k in range(PIECES[m]):
                lists[-1].append((m, k, rows, x_first))
    return lists


def exchange(shapes, n, *refs):
    refs = list(refs)

    def take(count):
        out, refs[:] = refs[:count], refs[count:]
        return out

    grads, weights, moments = take(6), take(6), take(6)
    norm_inputs = take(3)
    gathered, news, states = take(6), take(6), take(6)
    norm_pack, norm_out = take(2)
    grad_v, weight_v, moment_v, new_v, state_v = (take(6) for _ in range(5))
    send_1, recv_1, send_2, recv_2, keep_2 = (take(6) for _ in range(5))
    send_3, recv_3, keep_3, own_v = (take(6) for _ in range(4))
    norm_send, norm_recv, norm_all = take(3)
    norm_held = take(3)
    grad_norm, weight_norm, moment_norm = norm_held
    sems, param_sems, norm_sems, norm_sems_2, norm_sems_3 = take(5)

    me = lax.axis_index("batch")
    c = lax.rem(me, 2)
    x = lax.rem(lax.div(me, 2), 2)
    y = lax.div(me, 4)
    other_c, other_x, other_y = me + 1 - 2 * c, me + 2 - 4 * x, me + 4 - 8 * y
    rate = n ** (-0.5)

    lists = pieces_of(shapes)
    pairs = len(lists[0])
    number = {}
    for p in range(pairs):
        for s in range(2):
            number[lists[s][p][:2]] = 2 * p + s

    def sem(piece, kind):
        return sems.at[number[piece[:2]], kind]

    def load(piece):
        m, k, rows, _ = piece
        at = pl.ds(k * rows, rows)
        if BY_ROWS[m]:
            source, target = grads[m].at[:, at, :], grad_v[m].at[:, at, :]
        else:
            source, target = grads[m].at[at, :], grad_v[m].at[at, :]
        return pltpu.make_async_copy(source, target, sem(piece, LOAD))

    def params(m):
        return (
            pltpu.make_async_copy(weights[m], weight_v[m], param_sems.at[m, 0]),
            pltpu.make_async_copy(moments[m], moment_v[m], param_sems.at[m, 1]),
        )

    def remote(piece, step, source, target, device):
        return pltpu.make_async_remote_copy(
            src_ref=source,
            dst_ref=target,
            send_sem=sem(piece, SEND + step),
            recv_sem=sem(piece, RECV + step),
            device_id={"batch": device},
            device_id_type=pl.DeviceIdType.MESH,
        )

    def hop(piece, step):
        m, k, rows, x_first = piece
        first, second = (other_x, other_y) if x_first else (other_y, other_x)
        place = gathered[m]
        if step == 0:
            return remote(piece, 0, send_1[m].at[k], recv_1[m].at[k], other_c)
        if step == 1:
            return remote(piece, 1, send_2[m].at[k], recv_2[m].at[k], first)
        if step == 2:
            return remote(piece, 2, send_3[m].at[k], recv_3[m].at[k], second)
        if step == 3:
            return remote(piece, 3, own_v[m].at[k], place.at[k, y, x, c], second)
        if step == 4:
            part = place.at[k, :, x, c] if x_first else place.at[k, y, :, c]
            return remote(piece, 4, part, part, first)
        part = place.at[k, :, :, c]
        return remote(piece, 5, part, part, other_c)

    def own_copies(piece):
        m, k, rows, _ = piece
        at = pl.ds(k * rows, rows)
        return (
            pltpu.make_async_copy(own_v[m].at[k], gathered[m].at[k, y, x, c], sem(piece, OWN)),
            pltpu.make_async_copy(new_v[m].at[at, :], news[m].at[at, :], sem(piece, NEW)),
            pltpu.make_async_copy(state_v[m].at[at, :], states[m].at[at, :], sem(piece, STATE)),
        )

    def block(piece, owner):
        m, k, rows, _ = piece
        at = pl.ds(k * rows, rows)
        if BY_ROWS[m]:
            return grad_v[m][owner, at, :]
        width = shapes[m][1]
        return grad_v[m][at, pl.ds(pl.multiple_of(owner * width, width), width)]

    def stage(piece, step):
        m, k, rows, x_first = piece
        f, s = (x, y) if x_first else (y, x)

        def spot(first, second):
            return 2 * second + first if x_first else 2 * first + second

        if step == 0:
            load(piece).wait()
            for q in range(4):
                send_1[m][k, q] = block(piece, 2 * q + 1 - c).astype(jnp.bfloat16)
            hop(piece, 0).start()
        elif step == 1:
            hop(piece, 0).wait_recv()
            for second in range(2):
                q = spot(1 - f, second)
                total = block(piece, 2 * q + c) + recv_1[m][k, q].astype(jnp.float32)
                send_2[m][k, second] = total.astype(jnp.bfloat16)
            hop(piece, 1).start()
            for second in range(2):
                q = spot(f, second)
                keep_2[m][k, second] = block(piece, 2 * q + c) + recv_1[m][k, q].astype(jnp.float32)
        elif step == 2:
            hop(piece, 1).wait_recv()
            total = keep_2[m][k, 1 - s] + recv_2[m][k, 1 - s].astype(jnp.float32)
            send_3[m][k] = total.astype(jnp.bfloat16)
            hop(piece, 2).start()
            keep_3[m][k] = keep_2[m][k, s] + recv_2[m][k, s].astype(jnp.float32)
        elif step == 3:
            if k == 0:
                for copy in params(m):
                    copy.wait()
            hop(piece, 2).wait_recv()
            at = pl.ds(k * rows, rows)
            mean = (keep_3[m][k] + recv_3[m][k].astype(jnp.float32)) * rate
            state = hold_rate * moment_v[m][at, :] + mean
            new = weight_v[m][at, :] - learn_rate * state
            own_v[m][k] = new.astype(jnp.bfloat16)
            hop(piece, 3).start()
            new_v[m][at, :] = new
            state_v[m][at, :] = state
            for copy in own_copies(piece):
                copy.start()
        elif step == 4:
            own_copies(piece)[0].wait()
            hop(piece, 3).wait_recv()
            hop(piece, 4).start()
        elif step == 5:
            hop(piece, 4).wait_recv()
            hop(piece, 5).start()
        else:
            hop(piece, 5).wait_recv()

    started = set()
    for p in range(pairs):
        for s in range(2):
            load(lists[s][p]).start()
        if p >= 1:
            for s in range(2):
                m = lists[s][p - 1][0]
                if m not in started:
                    started.add(m)
                    for copy in params(m):
                        copy.start()
    for m in range(6):
        if m not in started:
            for copy in params(m):
                copy.start()

    barrier = pltpu.get_barrier_semaphore()
    for d in range(1, n):
        pl.semaphore_signal(
            barrier, inc=1, device_id={"batch": lax.rem(me + d, n)}, device_id_type=pl.DeviceIdType.MESH
        )
    pl.semaphore_wait(barrier, n - 1)

    width = weight_norm.shape[1]

    def norm_hop(d):
        to = lax.rem(me + d, n)
        return pltpu.make_async_remote_copy(
            src_ref=norm_send.at[to],
            dst_ref=norm_recv.at[d],
            send_sem=norm_sems.at[0, d],
            recv_sem=norm_sems.at[1, d],
            device_id={"batch": to},
            device_id_type=pl.DeviceIdType.MESH,
        )

    def norm_back(d):
        to = lax.rem(me + d, n)
        return pltpu.make_async_remote_copy(
            src_ref=norm_pack.at[0],
            dst_ref=norm_all.at[d],
            send_sem=norm_sems_2.at[0, d],
            recv_sem=norm_sems_2.at[1, d],
            device_id={"batch": to},
            device_id_type=pl.DeviceIdType.MESH,
        )

    def norm_loads():
        return [
            pltpu.make_async_copy(source, target, norm_sems_3.at[i])
            for i, (source, target) in enumerate(zip(norm_inputs, norm_held))
        ]

    def norm_start():
        for copy in norm_loads():
            copy.wait()
        for j in range(n):
            part = grad_norm[:, j * width : (j + 1) * width]
            norm_send[j] = jnp.broadcast_to(part, (8, width))
        for d in range(1, n):
            norm_hop(d).start()

    def norm_update():
        total = norm_send[me]
        for d in range(1, n):
            norm_hop(d).wait_recv()
            total = total + norm_recv[d]
        state = hold_rate * moment_norm[...] + total * rate
        norm_pack[1] = state
        norm_pack[0] = weight_norm[...] - learn_rate * state
        for d in range(1, n):
            norm_back(d).start()

    def norm_end():
        norm_out[me] = norm_pack[0]
        for d in range(1, n):
            norm_back(d).wait_recv()
            norm_out[lax.rem(me + n - d, n)] = norm_all[d]

    for copy in norm_loads():
        copy.start()
    for slot in range(pairs + DELAYS[-1]):
        for step in STEP_ORDER:
            p = slot - DELAYS[step]
            if 0 <= p < pairs:
                for s in range(2):
                    stage(lists[s][p], step)
        if slot == 1:
            norm_start()
        if slot == 3:
            norm_update()
    norm_end()

    for p in range(pairs):
        for s in range(2):
            piece = lists[s][p]
            for step in range(6):
                hop(piece, step).wait_send()
            for copy in own_copies(piece)[1:]:
                copy.wait()
    for d in range(1, n):
        norm_hop(d).wait_send()
        norm_back(d).wait_send()


def write_out(shapes, n, *refs):
    refs = list(refs)

    def take(count):
        out, refs[:] = refs[:count], refs[count:]
        return out

    gathered, news, states = take(6), take(6), take(6)
    norm_pack, norm_out = take(2)
    copies, new_outs, state_outs = take(6), take(6), take(6)
    copy_norm, new_norm, state_norm = take(3)
    (sems,) = take(1)
    started = []
    count = 0
    for m in range(6):
        rows = shapes[m][0] // PIECES[m]
        width = shapes[m][1]
        for k in range(PIECES[m]):
            for j in range(n):
                source = gathered[m].at[k, j // 4, j // 2 % 2, j % 2]
                if BY_ROWS[m]:
                    target = copies[m].at[pl.ds(j * shapes[m][0] + k * rows, rows), :]
                else:
                    target = copies[m].at[pl.ds(k * rows, rows), pl.ds(j * width, width)]
                started.append(pltpu.make_async_copy(source, target, sems.at[count]))
                count += 1
        for source, target in ((news[m], new_outs[m]), (states[m], state_outs[m])):
            started.append(pltpu.make_async_copy(source, target, sems.at[count]))
            count += 1
    for copy in started:
        copy.start()
    for j in range(n):
        width = norm_out.shape[2]
        copy_norm[:, j * width : (j + 1) * width] = norm_out[j, 0:1, :].astype(jnp.bfloat16)
    new_norm[...] = norm_pack[0, 0:1, :]
    state_norm[...] = norm_pack[1, 0:1, :]
    for copy in started:
        copy.wait()


def kernel_body(*args):
    n = lax.axis_size("batch")
    grads, grad_norm = [a[0] for a in args[:6]], args[6]
    weights, weight_norm = args[7:13], args[13]
    moments, moment_norm = args[14:20], args[20]
    shapes = [w.shape for w in weights]
    grads = [g.reshape((n, *s)) if by_rows else g for g, s, by_rows in zip(grads, shapes, BY_ROWS)]
    width = weight_norm.shape[0]
    bf16, f32 = jnp.bfloat16, jnp.float32
    any_spec = pl.BlockSpec(memory_space=pl.ANY)
    vmem_spec = pl.BlockSpec(memory_space=pltpu.VMEM)
    hbm_spec = pl.BlockSpec(memory_space=pltpu.HBM)

    def cut(m):
        rows, cols = shapes[m]
        return PIECES[m], rows // PIECES[m], cols

    every = range(6)

    def scratch(lead, kind):
        return [pltpu.VMEM((cut(m)[0], *lead, *cut(m)[1:]), kind) for m in every]

    whole = [pltpu.VMEM(s, f32) for s in shapes]
    held = [pltpu.VMEM((cut(m)[0], 2, 2, 2, *cut(m)[1:]), bf16) for m in every] + whole + whole
    lists = pieces_of(shapes)
    assert len(lists[0]) == len(lists[1])
    norms = (grad_norm, weight_norm.reshape(1, width), moment_norm.reshape(1, width))
    arrays = (*grads, *weights, *moments, *norms)
    results = pl.pallas_call(
        functools.partial(exchange, shapes, n),
        out_shape=held
        + [jax.ShapeDtypeStruct((2, 8, width), f32), jax.ShapeDtypeStruct((n, 8, width), f32)],
        in_specs=[any_spec] * 21,
        out_specs=[any_spec] * 18 + [vmem_spec] * 2,
        scratch_shapes=[pltpu.VMEM(g.shape, f32) for g in grads]
        + whole * 4
        + scratch((4,), bf16) * 2
        + scratch((2,), bf16) * 2
        + scratch((2,), f32)
        + scratch((), bf16) * 2
        + scratch((), f32)
        + scratch((), bf16)
        + [pltpu.VMEM((n, 8, width), f32)] * 3
        + [pltpu.VMEM((1, n * width), f32)]
        + [pltpu.VMEM((1, width), f32)] * 2
        + [
            pltpu.SemaphoreType.DMA((2 * len(lists[0]), KINDS)),
            pltpu.SemaphoreType.DMA((6, 2)),
            pltpu.SemaphoreType.DMA((2, n)),
            pltpu.SemaphoreType.DMA((2, n)),
            pltpu.SemaphoreType.DMA((3,)),
        ],
        compiler_params=pltpu.CompilerParams(
            collective_id=0, has_side_effects=True, vmem_limit_bytes=40 * 2**20
        ),
    )(*[pltpu.with_memory_space_constraint(a, pltpu.HBM) for a in arrays])
    copies = n * sum(PIECES) + 12
    finals = pl.pallas_call(
        functools.partial(write_out, shapes, n),
        out_shape=[
            jax.ShapeDtypeStruct((n * s[0], s[1]) if by_rows else (s[0], n * s[1]), bf16)
            for s, by_rows in zip(shapes, BY_ROWS)
        ]
        + [jax.ShapeDtypeStruct(s, f32) for s in shapes] * 2
        + [
            jax.ShapeDtypeStruct((1, n * width), bf16),
            jax.ShapeDtypeStruct((1, width), f32),
            jax.ShapeDtypeStruct((1, width), f32),
        ],
        in_specs=[any_spec] * 18 + [vmem_spec] * 2,
        out_specs=[hbm_spec] * 18 + [vmem_spec] * 3,
        scratch_shapes=[pltpu.SemaphoreType.DMA((copies,))],
        compiler_params=pltpu.CompilerParams(vmem_limit_bytes=8 * 2**20),
    )(*[pltpu.with_memory_space_constraint(r, pltpu.VMEM) for r in results[:18]], *results[18:])
    copy, new, state = finals[:6], finals[6:12], finals[12:18]
    copy_norm, new_norm, state_norm = (r.reshape(r.shape[1]) for r in finals[18:])
    return (*copy, copy_norm, *new, new_norm, *state, state_norm)


def chosen(*args):
    fits = lax.axis_size("batch") == 2**3 and args[13].shape[0] % 128 == 0
    for w, count in zip(args[7:13], PIECES):
        fits = fits and w.shape[0] % (16 * count) == 0 and w.shape[1] % 128 == 0
    return kernel_body(*args) if fits else body(*args)


def solution(mesh):
    in_specs = (
        P("batch", None, "cols"),
        P("batch", "cols", None),
        P("batch", None, "cols"),
        P("batch", None, "cols"),
        P("batch", None, "cols"),
        P("batch", "cols", None),
        P("batch", None),
        P("batch", "cols"),
        P("cols", "batch"),
        P("batch", "cols"),
        P("batch", "cols"),
        P("batch", "cols"),
        P("cols", "batch"),
        P("batch"),
        P("batch", "cols"),
        P("cols", "batch"),
        P("batch", "cols"),
        P("batch", "cols"),
        P("batch", "cols"),
        P("cols", "batch"),
        P("batch"),
    )
    out_specs = (
        P(None, "cols"),
        P("cols", None),
        P(None, "cols"),
        P(None, "cols"),
        P(None, "cols"),
        P("cols", None),
        P(),
        P("batch", "cols"),
        P("cols", "batch"),
        P("batch", "cols"),
        P("batch", "cols"),
        P("batch", "cols"),
        P("cols", "batch"),
        P("batch"),
        P("batch", "cols"),
        P("cols", "batch"),
        P("batch", "cols"),
        P("batch", "cols"),
        P("batch", "cols"),
        P("cols", "batch"),
        P("batch"),
    )
    return jax.shard_map(chosen, mesh=mesh, in_specs=in_specs, out_specs=out_specs, check_vma=False)
```

profile of v0, /device:TPU:0, one launch (start us, length us, event | category | flops | bytes accessed | tf_op | source)
XLA Modules:
  0.0 68.4 jit_solution(16261828131372978555)
XLA Ops:
  0.7 62.1 %shard_map.364 = (bf16[4,2,2,2,32,1024]{5,4,3,2,1,0:T(8,128)(2,1)S(1)}, bf16[4,2,2,2,256,128]{5,4,3,2,1,0:T(8,128)(2,1)S(1)}, bf16[1,2,2,2,128,256]{5,4,3,2,1,0:...) custom-call(f32[8,128,1024]{2,1,0:T(8,128)} %bitcast.10, ...), custom_call_target="tpu_custom_call" | custom-call | tf_op jit(solution)/shard_map/pallas_call | solution.py:460
  62.8 5.1 %shard_map.365 = (bf16[1024,1024]{1,0:T(8,128)(2,1)}, bf16[1024,1024]{1,0:T(8,128)(2,1)}, bf16[1024,256]{1,0:T(8,128)(2,1)}, bf16[1024,256]{1,0:T(8,128)(2,1)}, ...) custom-call(bf16[4,2,2,2,32,1024]{5,4,3,2,1,0:T(8,128)(2,1)S(1)} %ge, ...), custom_call_target="tpu_custom_call" | custom-call | tf_op jit(solution)/shard_map/pallas_call | solution.py:489
  67.8 0.6 reduce
where the time goes:
time: 68.7 us; the launch traced here: 68.4 us
  Pallas kernels  67.2 us (98%)
    pallas_call x1, Pallas kernels, kernel_body(): pl.pallas_call(functools.partial(exchange, shapes, n), out_shape=held + [...  62.1 us
    pallas_call x1, Pallas kernels, kernel_body(): pl.pallas_call(functools.partial(write_out, shapes, n), out_shape=[jax.Sh...  5.07 us

commit v1 on v0

v1 whole, which is shorter than its diff:
```python
import functools

import jax
import jax.numpy as jnp
from jax import lax
from jax.experimental import pallas as pl
from jax.experimental.pallas import tpu as pltpu
from jax.sharding import PartitionSpec as P

learn_rate = 0.1
hold_rate = 0.7


def body(
    grad_up,
    grad_down,
    grad_query,
    grad_key,
    grad_value,
    grad_mixed,
    grad_norm,
    weight_up,
    weight_down,
    weight_query,
    weight_key,
    weight_value,
    weight_mixed,
    weight_norm,
    moment_up,
    moment_down,
    moment_query,
    moment_key,
    moment_value,
    moment_mixed,
    moment_norm,
):
    mean_up, mean_down, mean_query, mean_key, mean_value, mean_mixed = (
        lax.psum_scatter(
            grad_up[0].astype(jnp.bfloat16), "batch", scatter_dimension=0, tiled=True
        ).astype(jnp.float32),
        lax.psum_scatter(
            grad_down[0].astype(jnp.bfloat16), "batch", scatter_dimension=1, tiled=True
        ).astype(jnp.float32),
        lax.psum_scatter(
            grad_query[0].astype(jnp.bfloat16), "batch", scatter_dimension=0, tiled=True
        ).astype(jnp.float32),
        lax.psum_scatter(
            grad_key[0].astype(jnp.bfloat16), "batch", scatter_dimension=0, tiled=True
        ).astype(jnp.float32),
        lax.psum_scatter(
            grad_value[0].astype(jnp.bfloat16), "batch", scatter_dimension=0, tiled=True
        ).astype(jnp.float32),
        lax.psum_scatter(
            grad_mixed[0].astype(jnp.bfloat16), "batch", scatter_dimension=1, tiled=True
        ).astype(jnp.float32),
    )
    whole_norm = lax.psum(grad_norm[0], "batch")
    place = lax.axis_index("batch")
    mean_norm = lax.dynamic_slice_in_dim(
        whole_norm, place * weight_norm.shape[0], weight_norm.shape[0]
    )
    mean_rate = lax.axis_size("batch") ** (-0.5)
    mean_up = mean_up * mean_rate
    mean_down = mean_down * mean_rate
    mean_query = mean_query * mean_rate
    mean_key = mean_key * mean_rate
    mean_value = mean_value * mean_rate
    mean_mixed = mean_mixed * mean_rate
    mean_norm = mean_norm * mean_rate
    state_new_up = hold_rate * moment_up + mean_up
    new_up = weight_up - learn_rate * state_new_up
    state_new_down = hold_rate * moment_down + mean_down
    new_down = weight_down - learn_rate * state_new_down
    state_new_query = hold_rate * moment_query + mean_query
    new_query = weight_query - learn_rate * state_new_query
    state_new_key = hold_rate * moment_key + mean_key
    new_key = weight_key - learn_rate * state_new_key
    state_new_value = hold_rate * moment_value + mean_value
    new_value = weight_value - learn_rate * state_new_value
    state_new_mixed = hold_rate * moment_mixed + mean_mixed
    new_mixed = weight_mixed - learn_rate * state_new_mixed
    state_new_norm = hold_rate * moment_norm + mean_norm
    new_norm = weight_norm - learn_rate * state_new_norm
    copy_up, copy_down, copy_query, copy_key, copy_value, copy_mixed, copy_norm = (
        lax.all_gather(new_up.astype(jnp.bfloat16), "batch", axis=0, tiled=True),
        lax.all_gather(new_down.astype(jnp.bfloat16), "batch", axis=1, tiled=True),
        lax.all_gather(new_query.astype(jnp.bfloat16), "batch", axis=0, tiled=True),
        lax.all_gather(new_key.astype(jnp.bfloat16), "batch", axis=0, tiled=True),
        lax.all_gather(new_value.astype(jnp.bfloat16), "batch", axis=0, tiled=True),
        lax.all_gather(new_mixed.astype(jnp.bfloat16), "batch", axis=1, tiled=True),
        lax.all_gather(new_norm.astype(jnp.bfloat16), "batch", axis=0, tiled=True),
    )
    return (
        copy_up,
        copy_down,
        copy_query,
        copy_key,
        copy_value,
        copy_mixed,
        copy_norm,
        new_up,
        new_down,
        new_query,
        new_key,
        new_value,
        new_mixed,
        new_norm,
        state_new_up,
        state_new_down,
        state_new_query,
        state_new_key,
        state_new_value,
        state_new_mixed,
        state_new_norm,
    )


PLANS = (((2, (1, 1)), (0, (1, 1)), (3, (1, 1))), ((4, (1,1)), (1, (1, 1)), (5, (1, 1))))
AHEAD = 1
BY_ROWS = (True, False, True, True, True, False)
LOAD, SEND, RECV, KINDS = 0, 1, 7, 13


def pieces_of(shapes):
    lists = []
    for s, plan in enumerate(PLANS):
        lists.append([])
        for m, shares in plan:
            row = 0
            for share in shares:
                rows = shapes[m][0] * share // sum(shares)
                lists[s].append((2 * len(lists[s]) + s, m, row, rows, s == 0))
                row += rows
    return lists


def exchange(shapes, n, *refs):
    refs = list(refs)

    def take(count):
        out, refs[:] = refs[:count], refs[count:]
        return out

    lists = pieces_of(shapes)
    pairs = len(lists[0])
    grads, weights, moments = take(6), take(6), take(6)
    norm_inputs = take(3)
    gathered, news, states = take(6), take(6), take(6)
    norm_copy, norm_new, norm_state = take(3)
    grad_v, weight_v, moment_v = (take(6) for _ in range(3))
    send_1, recv_1, send_2, recv_2, keep_2 = (take(2 * pairs) for _ in range(5))
    send_3, recv_3, keep_3 = (take(2 * pairs) for _ in range(3))
    norm_held = take(3)
    norm_send, norm_recv, norm_full = take(3)
    sems, param_sems, norm_sems, norm_load_sems = take(4)

    me = lax.axis_index("batch")
    c = lax.rem(me, 2)
    x = lax.rem(lax.div(me, 2), 2)
    y = lax.div(me, 4)
    other_c, other_x, other_y = me + 1 - 2 * c, me + 2 - 4 * x, me + 4 - 8 * y
    rate = n ** (-0.5)

    barrier = pltpu.get_barrier_semaphore()
    for device in (other_c, other_x, other_y):
        pl.semaphore_signal(
            barrier, inc=1, device_id={"batch": device}, device_id_type=pl.DeviceIdType.MESH
        )

    def load(piece):
        i, m, row, rows, _ = piece
        at = pl.ds(row, rows)
        if BY_ROWS[m]:
            source, target = grads[m].at[:, at, :], grad_v[m].at[:, at, :]
        else:
            source, target = grads[m].at[at, :], grad_v[m].at[at, :]
        return pltpu.make_async_copy(source, target, sems.at[i, LOAD])

    def params(m):
        return (
            pltpu.make_async_copy(weights[m], weight_v[m], param_sems.at[m, 0]),
            pltpu.make_async_copy(moments[m], moment_v[m], param_sems.at[m, 1]),
        )

    def remote(source, target, send_sem, recv_sem, device):
        return pltpu.make_async_remote_copy(
            src_ref=source,
            dst_ref=target,
            send_sem=send_sem,
            recv_sem=recv_sem,
            device_id={"batch": device},
            device_id_type=pl.DeviceIdType.MESH,
        )

    def hop(piece, step):
        i, m, row, rows, x_first = piece
        first, second = (other_x, other_y) if x_first else (other_y, other_x)
        at = pl.ds(row, rows)
        place = gathered[m]
        if step == 0:
            source, target, device = send_1[i], recv_1[i], other_c
        elif step == 1:
            source, target, device = send_2[i], recv_2[i], first
        elif step == 2:
            source, target, device = send_3[i], recv_3[i], second
        else:
            if step == 3:
                part, device = place.at[y, x, c, at, :], second
            elif step == 4:
                part = place.at[:, x, c, at, :] if x_first else place.at[y, :, c, at, :]
                device = first
            else:
                part, device = place.at[:, :, c, at, :], other_c
            source = target = part
        return remote(source, target, sems.at[i, SEND + step], sems.at[i, RECV + step], device)

    def block(piece, owner):
        _, m, row, rows, _ = piece
        at = pl.ds(row, rows)
        if BY_ROWS[m]:
            return grad_v[m][owner, at, :]
        width = shapes[m][1]
        return grad_v[m][at, pl.ds(pl.multiple_of(owner * width, width), width)]

    waited = set()

    def stage(piece, step):
        i, m, row, rows, x_first = piece
        f, s = (x, y) if x_first else (y, x)
        at = pl.ds(row, rows)

        def spot(first, second):
            return 2 * second + first if x_first else 2 * first + second

        if step == 0:
            load(piece).wait()
            for q in range(4):
                send_1[i][q] = block(piece, 2 * q + 1 - c).astype(jnp.bfloat16)
            hop(piece, 0).start()
        elif step == 1:
            hop(piece, 0).wait_recv()
            for second in range(2):
                q = spot(1 - f, second)
                total = block(piece, 2 * q + c) + recv_1[i][q].astype(jnp.float32)
                send_2[i][second] = total.astype(jnp.bfloat16)
            hop(piece, 1).start()
            for second in range(2):
                q = spot(f, second)
                keep_2[i][second] = block(piece, 2 * q + c) + recv_1[i][q].astype(jnp.float32)
        elif step == 2:
            hop(piece, 1).wait_recv()
            total = keep_2[i][1 - s] + recv_2[i][1 - s].astype(jnp.float32)
            send_3[i][...] = total.astype(jnp.bfloat16)
            hop(piece, 2).start()
            keep_3[i][...] = keep_2[i][s] + recv_2[i][s].astype(jnp.float32)
            hop(piece, 0).wait_send()
        elif step == 3:
            if m not in waited:
                waited.add(m)
                for copy in params(m):
                    copy.wait()
            hop(piece, 2).wait_recv()
            mean = (keep_3[i][...] + recv_3[i][...].astype(jnp.float32)) * rate
            state = hold_rate * moment_v[m][at, :] + mean
            new = weight_v[m][at, :] - learn_rate * state
            gathered[m][y, x, c, at, :] = new.astype(jnp.bfloat16)
            hop(piece, 3).start()
            news[m][at, :] = new
            states[m][at, :] = state
            hop(piece, 1).wait_send()
        elif step == 4:
            hop(piece, 3).wait_recv()
            hop(piece, 4).start()
            hop(piece, 2).wait_send()
        elif step == 5:
            hop(piece, 4).wait_recv()
            hop(piece, 5).start()
            hop(piece, 3).wait_send()
        else:
            hop(piece, 5).wait_recv()
            hop(piece, 4).wait_send()
            hop(piece, 5).wait_send()

    def both(step, p):
        for s in range(2):
            stage(lists[s][p], step)

    def norm_loads():
        return [
            pltpu.make_async_copy(source, target, norm_load_sems.at[i])
            for i, (source, target) in enumerate(zip(norm_inputs, norm_held))
        ]

    def norm_hop(step):
        device = (other_c, other_x, other_y)[step]
        return remote(
            norm_send.at[step], norm_recv.at[step], norm_sems.at[0, step], norm_sems.at[1, step], device
        )

    def norm_stage(step):
        width = norm_held[1].shape[1]
        if step == 0:
            for copy in norm_loads():
                copy.wait()
            for j in range(n):
                norm_send[0, 0, pl.ds(j, 1), :] = norm_held[0][:, j * width : (j + 1) * width]
            own = lax.broadcasted_iota(jnp.int32, (n, width), 0) == me
            for j in (1, 2):
                norm_send[0, j] = jnp.where(own, jnp.broadcast_to(norm_held[j][...], (n, width)), 0.0)
            norm_hop(0).start()
            return
        norm_hop(step - 1).wait_recv()
        total = norm_send[step - 1] + norm_recv[step - 1]
        if step < 3:
            norm_send[step] = total
            norm_hop(step).start()
            return
        state = hold_rate * total[2] + total[0] * rate
        new = total[1] - learn_rate * state
        norm_copy[...] = new.astype(jnp.bfloat16)
        norm_full[0] = new
        norm_full[1] = state
        norm_new[...] = norm_full[0, pl.ds(me, 1), :]
        norm_state[...] = norm_full[1, pl.ds(me, 1), :]
        for i in range(3):
            norm_hop(i).wait_send()

    for p in range(pairs):
        for s in range(2):
            load(lists[s][p]).start()
        if p == AHEAD:
            for copy in norm_loads():
                copy.start()
    for m in dict.fromkeys(m for pair in zip(*PLANS) for m, _ in pair):
        for copy in params(m):
            copy.start()
    pl.semaphore_wait(barrier, 3)

    for p in range(pairs + AHEAD):
        if p < pairs:
            both(0, p)
        if p >= AHEAD:
            both(1, p - AHEAD)
        if p == AHEAD + 1:
            norm_stage(0)
    norm_stage(1)
    for p in range(pairs):
        both(2, p)
    norm_stage(2)
    for p in range(pairs):
        both(3, p)
    norm_stage(3)
    for step in (4, 5, 6):
        for p in range(pairs):
            both(step, p)


def write_out(shapes, n, *refs):
    refs = list(refs)

    def take(count):
        out, refs[:] = refs[:count], refs[count:]
        return out

    gathered, plain_in = take(6), take(15)
    copies, plain_out = take(6), take(15)
    (sems,) = take(1)
    moves = []
    for m in range(6):
        if BY_ROWS[m]:
            moves.append((gathered[m], copies[m]))
            continue
        width = shapes[m][1]
        for j in range(n):
            source = gathered[m].at[j // 4, j // 2 % 2, j % 2]
            moves.append((source, copies[m].at[:, pl.ds(j * width, width)]))
    moves += zip(plain_in, plain_out)
    started = [pltpu.make_async_copy(a, b, sems.at[i]) for i, (a, b) in enumerate(moves)]
    for copy in started:
        copy.start()
    for copy in started:
        copy.wait()


def kernel_body(*args):
    n = lax.axis_size("batch")
    grads, grad_norm = [a[0] for a in args[:6]], args[6]
    weights, weight_norm = args[7:13], args[13]
    moments, moment_norm = args[14:20], args[20]
    shapes = [w.shape for w in weights]
    grads = [g.reshape((n, *s)) if by_rows else g for g, s, by_rows in zip(grads, shapes, BY_ROWS)]
    width = weight_norm.shape[0]
    bf16, f32 = jnp.bfloat16, jnp.float32
    any_spec = pl.BlockSpec(memory_space=pl.ANY)
    vmem_spec = pl.BlockSpec(memory_space=pltpu.VMEM)
    hbm_spec = pl.BlockSpec(memory_space=pltpu.HBM)
    lists = pieces_of(shapes)
    assert len(lists[0]) == len(lists[1])
    ordered = [piece for pair in zip(*lists) for piece in pair]

    def scratch(lead, kind):
        return [pltpu.VMEM((*lead, rows, shapes[m][1]), kind) for _, m, _, rows, _ in ordered]

    whole = [pltpu.VMEM(s, f32) for s in shapes]
    plain = [jax.ShapeDtypeStruct(s, f32) for s in shapes] * 2 + [
        jax.ShapeDtypeStruct((n, width), bf16),
        jax.ShapeDtypeStruct((1, width), f32),
        jax.ShapeDtypeStruct((1, width), f32),
    ]
    parts = [jax.ShapeDtypeStruct((2, 2, 2, *s), bf16) for s in shapes]
    norms = (grad_norm, weight_norm.reshape(1, width), moment_norm.reshape(1, width))
    arrays = (*grads, *weights, *moments, *norms)
    results = pl.pallas_call(
        functools.partial(exchange, shapes, n),
        out_shape=parts + plain,
        in_specs=[any_spec] * 21,
        out_specs=[vmem_spec] * 21,
        scratch_shapes=[pltpu.VMEM(g.shape, f32) for g in grads]
        + whole * 2
        + scratch((4,), bf16) * 2
        + scratch((2,), bf16) * 2
        + scratch((2,), f32)
        + scratch((), bf16) * 2
        + scratch((), f32)
        + [pltpu.VMEM((1, n * width), f32)]
        + [pltpu.VMEM((1, width), f32)] * 2
        + [pltpu.VMEM((3, 3, n, width), f32)] * 2
        + [pltpu.VMEM((2, n, width), f32)]
        + [
            pltpu.SemaphoreType.DMA((len(ordered), KINDS)),
            pltpu.SemaphoreType.DMA((6, 2)),
            pltpu.SemaphoreType.DMA((2, 3)),
            pltpu.SemaphoreType.DMA((3,)),
        ],
        compiler_params=pltpu.CompilerParams(
            collective_id=0, has_side_effects=True, vmem_limit_bytes=40 * 2**20
        ),
    )(*[pltpu.with_memory_space_constraint(a, pltpu.HBM) for a in arrays])
    columns = sum(not by_rows for by_rows in BY_ROWS)
    finals = pl.pallas_call(
        functools.partial(write_out, shapes, n),
        out_shape=[
            part if by_rows else jax.ShapeDtypeStruct((s[0], n * s[1]), bf16)
            for part, s, by_rows in zip(parts, shapes, BY_ROWS)
        ]
        + plain,
        in_specs=[any_spec] * 21,
        out_specs=[hbm_spec] * 21,
        scratch_shapes=[pltpu.SemaphoreType.DMA((21 + columns * (n - 1),))],
        compiler_params=pltpu.CompilerParams(vmem_limit_bytes=8 * 2**20),
    )(*[pltpu.with_memory_space_constraint(r, pltpu.VMEM) for r in results])
    copy = [f.reshape(-1, f.shape[-1]) for f in finals[:6]]
    new, state = finals[6:12], finals[12:18]
    copy_norm, new_norm, state_norm = (r.reshape(-1) for r in finals[18:])
    return (*copy, copy_norm, *new, new_norm, *state, state_norm)


def chosen(*args):
    fits = lax.axis_size("batch") == 2**3 and args[13].shape[0] % 128 == 0
    for m, shares in PLANS[0] + PLANS[1]:
        w = args[7 + m]
        fits = fits and w.shape[0] % (16 * sum(shares)) == 0 and w.shape[1] % 128 == 0
    return kernel_body(*args) if fits else body(*args)


def solution(mesh):
    in_specs = (
        P("batch", None, "cols"),
        P("batch", "cols", None),
        P("batch", None, "cols"),
        P("batch", None, "cols"),
        P("batch", None, "cols"),
        P("batch", "cols", None),
        P("batch", None),
        P("batch", "cols"),
        P("cols", "batch"),
        P("batch", "cols"),
        P("batch", "cols"),
        P("batch", "cols"),
        P("cols", "batch"),
        P("batch"),
        P("batch", "cols"),
        P("cols", "batch"),
        P("batch", "cols"),
        P("batch", "cols"),
        P("batch", "cols"),
        P("cols", "batch"),
        P("batch"),
    )
    out_specs = (
        P(None, "cols"),
        P("cols", None),
        P(None, "cols"),
        P(None, "cols"),
        P(None, "cols"),
        P("cols", None),
        P(),
        P("batch", "cols"),
        P("cols", "batch"),
        P("batch", "cols"),
        P("batch", "cols"),
        P("batch", "cols"),
        P("cols", "batch"),
        P("batch"),
        P("batch", "cols"),
        P("cols", "batch"),
        P("batch", "cols"),
        P("batch", "cols"),
        P("batch", "cols"),
        P("cols", "batch"),
        P("batch"),
    )
    return jax.shard_map(chosen, mesh=mesh, in_specs=in_specs, out_specs=out_specs, check_vma=False)
```

time: 68.7 us -> 64.9 us (0.945)
  Pallas kernels: 67.2 us -> 64 us
    pallas_call x2, Pallas kernels: 67.2 us -> 64 us  [the longest x1 60.1 us: kernel_body(): pl.pallas_call(functools.partial(exchange, shapes, n), out_shape=parts +...]
where the time goes in v1:
time: 64.9 us; the launch traced here: 64.7 us
  Pallas kernels  64 us (99%)
  between operations  0.67 us (1%)
    pallas_call x1, Pallas kernels, kernel_body(): pl.pallas_call(functools.partial(exchange, shapes, n), out_shape=parts +...  60.1 us
    pallas_call x1, Pallas kernels, kernel_body(): pl.pallas_call(functools.partial(write_out, shapes, n), out_shape=[part i...  3.91 us

profile of v1, /device:TPU:0, one launch (start us, length us, event | category | flops | bytes accessed | tf_op | source)
XLA Modules:
  0.0 64.7 jit_solution(930395953036159077)
XLA Ops:
  0.7 60.1 %shard_map.364 = (bf16[2,2,2,128,1024]{4,3,2,1,0:T(8,128)(2,1)S(1)}, bf16[2,2,2,1024,128]{4,3,2,1,0:T(8,128)(2,1)S(1)}, bf16[2,2,2,128,256]{4,3,2,1,0:T(8,128)(2...) custom-call(f32[8,128,1024]{2,1,0:T(8,128)} %bitcast.15, ...), custom_call_target="tpu_custom_call" | custom-call | tf_op jit(solution)/shard_map/pallas_call | solution.py:413
  60.8 3.9 %shard_map.365 = (bf16[2,2,2,128,1024]{4,3,2,1,0:T(8,128)(2,1)}, bf16[1024,1024]{1,0:T(8,128)(2,1)}, bf16[2,2,2,128,256]{4,3,2,1,0:T(8,128)(2,1)}, bf16[2,2,2,12...) custom-call(bf16[2,2,2,128,1024]{4,3,2,1,0:T(8,128)(2,1)S(1)} %get-t, ...), custom_call_target="tpu_custom_call" | custom-call | tf_op jit(solution)/shard_map/pallas_call | solution.py:440

commit v2 on v1

--- a/solution.py
+++ b/solution.py
@@ -115,22 +115,30 @@
     )
 
 
-PLANS = (((2, (1, 1)), (0, (1, 1)), (3, (1, 1))), ((4, (1,1)), (1, (1, 1)), (5, (1, 1))))
-AHEAD = 1
+PLANS = (
+    ((2, ((1, 3),)), (0, ((1, 1), (2,))), (3, ((1, 1),))),
+    ((4, ((1, 3),)), (1, ((1, 1), (2,))), (5, ((1, 1),))),
+)
+LEAD = 2
 BY_ROWS = (True, False, True, True, True, False)
-LOAD, SEND, RECV, KINDS = 0, 1, 7, 13
+LOAD, CORE, FIRST, KINDS = 0, 1, 2, 3
 
 
 def pieces_of(shapes):
     lists = []
+    count = 0
     for s, plan in enumerate(PLANS):
         lists.append([])
         for m, shares in plan:
             row = 0
-            for share in shares:
-                rows = shapes[m][0] * share // sum(shares)
-                lists[s].append((2 * len(lists[s]) + s, m, row, rows, s == 0))
-                row += rows
+            unit = shapes[m][0] // sum(map(sum, shares))
+            for group in shares:
+                start, pieces = row, []
+                for share in group:
+                    pieces.append((count, m, row, unit * share, s == 0))
+                    row += unit * share
+                    count += 1
+                lists[s].append((2 * len(lists[s]) + s, m, start, row - start, s == 0, pieces))
     return lists
 
 
@@ -142,17 +150,20 @@
         return out
 
     lists = pieces_of(shapes)
-    pairs = len(lists[0])
+    groups = len(lists[0])
+    streams = [[piece for group in groups_s for piece in group[-1]] for groups_s in lists]
+    pairs = len(streams[0])
+    early = [piece[0] for pair in zip(*streams) for piece in pair]
     grads, weights, moments = take(6), take(6), take(6)
     norm_inputs = take(3)
     gathered, news, states = take(6), take(6), take(6)
     norm_copy, norm_new, norm_state = take(3)
-    grad_v, weight_v, moment_v = (take(6) for _ in range(3))
+    grad_v, param_v = take(6), take(6)
     send_1, recv_1, send_2, recv_2, keep_2 = (take(2 * pairs) for _ in range(5))
-    send_3, recv_3, keep_3 = (take(2 * pairs) for _ in range(3))
+    send_3, recv_3, keep_3 = (take(2 * groups) for _ in range(3))
     norm_held = take(3)
     norm_send, norm_recv, norm_full = take(3)
-    sems, param_sems, norm_sems, norm_load_sems = take(4)
+    sems, send_sems, group_sems, norm_sems = take(4)
 
     me = lax.axis_index("batch")
     c = lax.rem(me, 2)
@@ -177,10 +188,14 @@
         return pltpu.make_async_copy(source, target, sems.at[i, LOAD])
 
     def params(m):
+        sem = sems.at[early[m], LOAD]
         return (
-            pltpu.make_async_copy(weights[m], weight_v[m], param_sems.at[m, 0]),
-            pltpu.make_async_copy(moments[m], moment_v[m], param_sems.at[m, 1]),
+            pltpu.make_async_copy(weights[m], param_v[m].at[0], sem),
+            pltpu.make_async_copy(moments[m], param_v[m].at[1], sem),
         )
+
+    def params_wait(m):
+        pltpu.make_async_copy(param_v[m], param_v[m], sems.at[early[m], LOAD]).wait()
 
     def remote(source, target, send_sem, recv_sem, device):
         return pltpu.make_async_remote_copy(
@@ -194,25 +209,30 @@
 
     def hop(piece, step):
         i, m, row, rows, x_first = piece
-        first, second = (other_x, other_y) if x_first else (other_y, other_x)
+        first = other_x if x_first else other_y
         at = pl.ds(row, rows)
         place = gathered[m]
-        if step == 0:
-            source, target, device = send_1[i], recv_1[i], other_c
-        elif step == 1:
-            source, target, device = send_2[i], recv_2[i], first
-        elif step == 2:
-            source, target, device = send_3[i], recv_3[i], second
-        else:
-            if step == 3:
-                part, device = place.at[y, x, c, at, :], second
-            elif step == 4:
-                part = place.at[:, x, c, at, :] if x_first else place.at[y, :, c, at, :]
-                device = first
-            else:
-                part, device = place.at[:, :, c, at, :], other_c
-            source = target = part
-        return remote(source, target, sems.at[i, SEND + step], sems.at[i, RECV + step], device)
+        half = place.at[:, x, c, at, :] if x_first else place.at[y, :, c, at, :]
+        source, target, device = (
+            (send_1[i], recv_1[i], other_c),
+            (send_2[i], recv_2[i], first),
+            (half, half, first),
+            (place.at[:, :, c, at, :], place.at[:, :, c, at, :], other_c),
+        )[step]
+        kind = (CORE, FIRST, LOAD, CORE)[step]
+        return remote(source, target, send_sems.at[m], sems.at[i, kind], device)
+
+    def group_hop(group, step):
+        g, m, row, rows, x_first, _ = group
+        second = other_y if x_first else other_x
+        place = gathered[m].at[y, x, c, pl.ds(row, rows), :]
+        source, target = ((send_3[g], recv_3[g]), (place, place))[step]
+        return remote(source, target, send_sems.at[m], group_sems.at[g, step], second)
+
+    def sent(m):
+        width = shapes[m][1]
+        part = pl.ds(0, 7) if BY_ROWS[m] else (slice(None), pl.ds(0, 7 * width))
+        pltpu.make_async_copy(grads[m].at[part], grad_v[m].at[part], send_sems.at[m]).wait()
 
     def block(piece, owner):
         _, m, row, rows, _ = piece
@@ -222,79 +242,74 @@
         width = shapes[m][1]
         return grad_v[m][at, pl.ds(pl.multiple_of(owner * width, width), width)]
 
-    waited = set()
-
-    def stage(piece, step):
-        i, m, row, rows, x_first = piece
-        f, s = (x, y) if x_first else (y, x)
+    def spot(x_first, first, second):
+        return 2 * second + first if x_first else 2 * first + second
+
+    def give(piece):
+        i = piece[0]
+        load(piece).wait()
+        for q in range(4):
+            send_1[i][q] = block(piece, 2 * q + 1 - c).astype(jnp.bfloat16)
+
+    def add_core(piece):
+        i, x_first = piece[0], piece[-1]
+        f = x if x_first else y
+        hop(piece, 0).wait_recv()
+        for second in range(2):
+            q = spot(x_first, 1 - f, second)
+            total = block(piece, 2 * q + c) + recv_1[i][q].astype(jnp.float32)
+            send_2[i][second] = total.astype(jnp.bfloat16)
+        hop(piece, 1).start()
+        for second in range(2):
+            q = spot(x_first, f, second)
+            keep_2[i][second] = block(piece, 2 * q + c) + recv_1[i][q].astype(jnp.float32)
+
+    def add_first(group):
+        g, m, start, _, x_first, pieces = group
+        s = y if x_first else x
+        for i, _, row, rows, _ in pieces:
+            hop((i, m, row, rows, x_first), 1).wait_recv()
+            total = keep_2[i][1 - s] + recv_2[i][1 - s].astype(jnp.float32)
+            send_3[g][pl.ds(row - start, rows), :] = total.astype(jnp.bfloat16)
+        group_hop(group, 0).start()
+        for i, _, row, rows, _ in pieces:
+            total = keep_2[i][s] + recv_2[i][s].astype(jnp.float32)
+            keep_3[g][pl.ds(row - start, rows), :] = total
+
+    def update(group):
+        g, m, row, rows, _, _ = group
         at = pl.ds(row, rows)
-
-        def spot(first, second):
-            return 2 * second + first if x_first else 2 * first + second
-
-        if step == 0:
-            load(piece).wait()
-            for q in range(4):
-                send_1[i][q] = block(piece, 2 * q + 1 - c).astype(jnp.bfloat16)
-            hop(piece, 0).start()
-        elif step == 1:
-            hop(piece, 0).wait_recv()
-            for second in range(2):
-                q = spot(1 - f, second)
-                total = block(piece, 2 * q + c) + recv_1[i][q].astype(jnp.float32)
-                send_2[i][second] = total.astype(jnp.bfloat16)
-            hop(piece, 1).start()
-            for second in range(2):
-                q = spot(f, second)
-                keep_2[i][second] = block(piece, 2 * q + c) + recv_1[i][q].astype(jnp.float32)
-        elif step == 2:
-            hop(piece, 1).wait_recv()
-            total = keep_2[i][1 - s] + recv_2[i][1 - s].astype(jnp.float32)
-            send_3[i][...] = total.astype(jnp.bfloat16)
+        group_hop(group, 0).wait_recv()
+        mean = (keep_3[g][...] + recv_3[g][...].astype(jnp.float32)) * rate
+        state = hold_rate * param_v[m][1, at, :] + mean
+        new = param_v[m][0, at, :] - learn_rate * state
+        gathered[m][y, x, c, at, :] = new.astype(jnp.bfloat16)
+        group_hop(group, 1).start()
+        news[m][at, :] = new
+        states[m][at, :] = state
+
+    def spread(group):
+        group_hop(group, 1).wait_recv()
+        for piece in group[-1]:
             hop(piece, 2).start()
-            keep_3[i][...] = keep_2[i][s] + recv_2[i][s].astype(jnp.float32)
-            hop(piece, 0).wait_send()
-        elif step == 3:
-            if m not in waited:
-                waited.add(m)
-                for copy in params(m):
-                    copy.wait()
-            hop(piece, 2).wait_recv()
-            mean = (keep_3[i][...] + recv_3[i][...].astype(jnp.float32)) * rate
-            state = hold_rate * moment_v[m][at, :] + mean
-            new = weight_v[m][at, :] - learn_rate * state
-            gathered[m][y, x, c, at, :] = new.astype(jnp.bfloat16)
-            hop(piece, 3).start()
-            news[m][at, :] = new
-            states[m][at, :] = state
-            hop(piece, 1).wait_send()
-        elif step == 4:
-            hop(piece, 3).wait_recv()
-            hop(piece, 4).start()
-            hop(piece, 2).wait_send()
-        elif step == 5:
-            hop(piece, 4).wait_recv()
-            hop(piece, 5).start()
-            hop(piece, 3).wait_send()
-        else:
-            hop(piece, 5).wait_recv()
-            hop(piece, 4).wait_send()
-            hop(piece, 5).wait_send()
-
-    def both(step, p):
-        for s in range(2):
-            stage(lists[s][p], step)
+
+    def pass_on(piece):
+        hop(piece, 2).wait_recv()
+        hop(piece, 3).start()
+
+    def finish(piece):
+        hop(piece, 3).wait_recv()
 
     def norm_loads():
         return [
-            pltpu.make_async_copy(source, target, norm_load_sems.at[i])
+            pltpu.make_async_copy(source, target, sems.at[early[6 + i], LOAD])
             for i, (source, target) in enumerate(zip(norm_inputs, norm_held))
         ]
 
     def norm_hop(step):
         device = (other_c, other_x, other_y)[step]
         return remote(
-            norm_send.at[step], norm_recv.at[step], norm_sems.at[0, step], norm_sems.at[1, step], device
+            norm_send.at[step], norm_recv.at[step], norm_sems.at[3], norm_sems.at[step], device
         )
 
     def norm_stage(step):
@@ -322,37 +337,50 @@
         norm_full[1] = state
         norm_new[...] = norm_full[0, pl.ds(me, 1), :]
         norm_state[...] = norm_full[1, pl.ds(me, 1), :]
-        for i in range(3):
-            norm_hop(i).wait_send()
-
-    for p in range(pairs):
-        for s in range(2):
-            load(lists[s][p]).start()
-        if p == AHEAD:
+        remote(norm_send, norm_recv, norm_sems.at[3], norm_sems.at[3], other_c).wait_send()
+
+    def both(act, parts):
+        for part in parts:
+            act(part)
+
+    in_pairs = list(zip(*streams))
+    group_pairs = list(zip(*lists))
+    for pair in in_pairs[: LEAD + 1]:
+        both(lambda piece: load(piece).start(), pair)
+    both(give, in_pairs[0])
+    pl.semaphore_wait(barrier, 3)
+    both(lambda piece: hop(piece, 0).start(), in_pairs[0])
+    for p in range(1, pairs + 1):
+        if p < pairs:
+            for piece in in_pairs[p]:
+                give(piece)
+                hop(piece, 0).start()
+        if p + LEAD < pairs:
+            both(lambda piece: load(piece).start(), in_pairs[p + LEAD])
+        if p == pairs - LEAD:
+            for m in range(6):
+                for copy in params(m):
+                    copy.start()
+        if p == pairs - 1:
             for copy in norm_loads():
                 copy.start()
-    for m in dict.fromkeys(m for pair in zip(*PLANS) for m, _ in pair):
-        for copy in params(m):
-            copy.start()
-    pl.semaphore_wait(barrier, 3)
-
-    for p in range(pairs + AHEAD):
-        if p < pairs:
-            both(0, p)
-        if p >= AHEAD:
-            both(1, p - AHEAD)
-        if p == AHEAD + 1:
-            norm_stage(0)
-    norm_stage(1)
-    for p in range(pairs):
-        both(2, p)
+        both(add_core, in_pairs[p - 1])
+    both(params_wait, range(6))
+    norm_stage(0)
+    for i, pair in enumerate(group_pairs):
+        both(add_first, pair)
+        if i == 0:
+            norm_stage(1)
     norm_stage(2)
-    for p in range(pairs):
-        both(3, p)
+    for pair in group_pairs:
+        both(update, pair)
     norm_stage(3)
-    for step in (4, 5, 6):
-        for p in range(pairs):
-            both(step, p)
+    for pair in group_pairs:
+        both(spread, pair)
+    for act in (pass_on, finish):
+        for pair in in_pairs:
+            both(act, pair)
+    both(sent, range(6))
 
 
 def write_out(shapes, n, *refs):
@@ -362,24 +390,32 @@
         out, refs[:] = refs[:count], refs[count:]
         return out
 
-    gathered, plain_in = take(6), take(15)
-    copies, plain_out = take(6), take(15)
-    (sems,) = take(1)
-    moves = []
+    gathered, news, states, norms = take(6), take(6), take(6), take(3)
+    copies, new_outs, state_outs, norm_outs = take(6), take(6), take(6), take(3)
+    sems, norm_sems = take(2)
     for m in range(6):
         if BY_ROWS[m]:
-            moves.append((gathered[m], copies[m]))
-            continue
-        width = shapes[m][1]
-        for j in range(n):
-            source = gathered[m].at[j // 4, j // 2 % 2, j % 2]
-            moves.append((source, copies[m].at[:, pl.ds(j * width, width)]))
-    moves += zip(plain_in, plain_out)
-    started = [pltpu.make_async_copy(a, b, sems.at[i]) for i, (a, b) in enumerate(moves)]
-    for copy in started:
-        copy.start()
-    for copy in started:
-        copy.wait()
+            pltpu.make_async_copy(gathered[m], copies[m], sems.at[m, 0]).start()
+        else:
+            width = shapes[m][1]
+            for j in range(n):
+                source = gathered[m].at[j // 4, j // 2 % 2, j % 2]
+                target = copies[m].at[:, pl.ds(j * width, width)]
+                pltpu.make_async_copy(source, target, sems.at[m, 0]).start()
+        pltpu.make_async_copy(news[m], new_outs[m], sems.at[m, 1]).start()
+        pltpu.make_async_copy(states[m], state_outs[m], sems.at[m, 1]).start()
+    moves = [
+        pltpu.make_async_copy(a, b, norm_sems.at[i])
+        for i, (a, b) in enumerate(zip(norms, norm_outs))
+    ]
+    for move in moves:
+        move.start()
+    for m in range(6):
+        every, half = gathered[m], gathered[m].at[0]
+        pltpu.make_async_copy(every, every, sems.at[m, 0]).wait()
+        pltpu.make_async_copy(half, half, sems.at[m, 1]).wait()
+    for move in moves:
+        move.wait()
 
 
 def kernel_body(*args):
@@ -395,13 +431,13 @@
     vmem_spec = pl.BlockSpec(memory_space=pltpu.VMEM)
     hbm_spec = pl.BlockSpec(memory_space=pltpu.HBM)
     lists = pieces_of(shapes)
-    assert len(lists[0]) == len(lists[1])
-    ordered = [piece for pair in zip(*lists) for piece in pair]
-
-    def scratch(lead, kind):
-        return [pltpu.VMEM((*lead, rows, shapes[m][1]), kind) for _, m, _, rows, _ in ordered]
-
-    whole = [pltpu.VMEM(s, f32) for s in shapes]
+    groups = [group for pair in zip(*lists) for group in pair]
+    pieces = [piece for groups_s in lists for group in groups_s for piece in group[-1]]
+    assert len(groups) == 2 * len(lists[0]) and len(groups) == 2 * len(lists[1])
+
+    def scratch(parts, lead, kind):
+        return [pltpu.VMEM((*lead, part[3], shapes[part[1]][1]), kind) for part in parts]
+
     plain = [jax.ShapeDtypeStruct(s, f32) for s in shapes] * 2 + [
         jax.ShapeDtypeStruct((n, width), bf16),
         jax.ShapeDtypeStruct((1, width), f32),
@@ -416,27 +452,26 @@
         in_specs=[any_spec] * 21,
         out_specs=[vmem_spec] * 21,
         scratch_shapes=[pltpu.VMEM(g.shape, f32) for g in grads]
-        + whole * 2
-        + scratch((4,), bf16) * 2
-        + scratch((2,), bf16) * 2
-        + scratch((2,), f32)
-        + scratch((), bf16) * 2
-        + scratch((), f32)
+        + [pltpu.VMEM((2, *s), f32) for s in shapes]
+        + scratch(pieces, (4,), bf16) * 2
+        + scratch(pieces, (2,), bf16) * 2
+        + scratch(pieces, (2,), f32)
+        + scratch(groups, (), bf16) * 2
+        + scratch(groups, (), f32)
         + [pltpu.VMEM((1, n * width), f32)]
         + [pltpu.VMEM((1, width), f32)] * 2
         + [pltpu.VMEM((3, 3, n, width), f32)] * 2
         + [pltpu.VMEM((2, n, width), f32)]
         + [
-            pltpu.SemaphoreType.DMA((len(ordered), KINDS)),
-            pltpu.SemaphoreType.DMA((6, 2)),
-            pltpu.SemaphoreType.DMA((2, 3)),
-            pltpu.SemaphoreType.DMA((3,)),
+            pltpu.SemaphoreType.DMA((len(pieces), KINDS)),
+            pltpu.SemaphoreType.DMA((6,)),
+            pltpu.SemaphoreType.DMA((len(groups), 2)),
+            pltpu.SemaphoreType.DMA((4,)),
         ],
         compiler_params=pltpu.CompilerParams(
             collective_id=0, has_side_effects=True, vmem_limit_bytes=40 * 2**20
         ),
     )(*[pltpu.with_memory_space_constraint(a, pltpu.HBM) for a in arrays])
-    columns = sum(not by_rows for by_rows in BY_ROWS)
     finals = pl.pallas_call(
         functools.partial(write_out, shapes, n),
         out_shape=[
@@ -446,7 +481,7 @@
         + plain,
         in_specs=[any_spec] * 21,
         out_specs=[hbm_spec] * 21,
-        scratch_shapes=[pltpu.SemaphoreType.DMA((21 + columns * (n - 1),))],
+        scratch_shapes=[pltpu.SemaphoreType.DMA((6, 2)), pltpu.SemaphoreType.DMA((3,))],
         compiler_params=pltpu.CompilerParams(vmem_limit_bytes=8 * 2**20),
     )(*[pltpu.with_memory_space_constraint(r, pltpu.VMEM) for r in results])
     copy = [f.reshape(-1, f.shape[-1]) for f in finals[:6]]
@@ -459,7 +494,7 @@
     fits = lax.axis_size("batch") == 2**3 and args[13].shape[0] % 128 == 0
     for m, shares in PLANS[0] + PLANS[1]:
         w = args[7 + m]
-        fits = fits and w.shape[0] % (16 * sum(shares)) == 0 and w.shape[1] % 128 == 0
+        fits = fits and w.shape[0] % (16 * sum(map(sum, shares))) == 0 and w.shape[1] % 128 == 0
     return kernel_body(*args) if fits else body(*args)
 
 

time: 64.9 us -> 63.6 us (0.980)
  Pallas kernels: 64 us -> 62.7 us
    pallas_call x1, Pallas kernels: 60.1 us -> 59 us  [kernel_body(): pl.pallas_call(functools.partial(exchange, shapes, n), out_shape=parts +...]
where the time goes in v2:
time: 63.6 us; the launch traced here: 63.4 us
  Pallas kernels  62.7 us (99%)
  between operations  0.67 us (1%)
    pallas_call x1, Pallas kernels, kernel_body(): pl.pallas_call(functools.partial(exchange, shapes, n), out_shape=parts +...  59 us
    pallas_call x1, Pallas kernels, kernel_body(): pl.pallas_call(functools.partial(write_out, shapes, n), out_shape=[part i...  3.74 us

profile of v2, /device:TPU:0, one launch (start us, length us, event | category | flops | bytes accessed | tf_op | source)
XLA Modules:
  0.0 63.4 jit_solution(16659537819111344196)
XLA Ops:
  0.7 59.0 %shard_map.364 = (bf16[2,2,2,128,1024]{4,3,2,1,0:T(8,128)(2,1)S(1)}, bf16[2,2,2,1024,128]{4,3,2,1,0:T(8,128)(2,1)S(1)}, bf16[2,2,2,128,256]{4,3,2,1,0:T(8,128)(2...) custom-call(f32[8,128,1024]{2,1,0:T(8,128)} %bitcast.15, ...), custom_call_target="tpu_custom_call" | custom-call | tf_op jit(solution)/shard_map/pallas_call | solution.py:449
  59.7 3.7 %shard_map.365 = (bf16[2,2,2,128,1024]{4,3,2,1,0:T(8,128)(2,1)}, bf16[1024,1024]{1,0:T(8,128)(2,1)}, bf16[2,2,2,128,256]{4,3,2,1,0:T(8,128)(2,1)}, bf16[2,2,2,12...) custom-call(bf16[2,2,2,128,1024]{4,3,2,1,0:T(8,128)(2,1)S(1)} %get-t, ...), custom_call_target="tpu_custom_call" | custom-call | tf_op jit(solution)/shard_map/pallas_call | solution.py:475

commit v3 on v2

--- a/solution.py
+++ b/solution.py
@@ -115,11 +115,9 @@
     )
 
 
-PLANS = (
-    ((2, ((1, 3),)), (0, ((1, 1), (2,))), (3, ((1, 1),))),
-    ((4, ((1, 3),)), (1, ((1, 1), (2,))), (5, ((1, 1),))),
-)
+PLANS = (((2, ((1, 3),)), (0, ((1, 1), (2,))), (3, ((3, 1),))), ((4, ((1, 3),)), (1, ((1, 1), (2,))), (5, ((3, 1),))))
 LEAD = 2
+LATE = 4
 BY_ROWS = (True, False, True, True, True, False)
 LOAD, CORE, FIRST, KINDS = 0, 1, 2, 3
 
@@ -153,6 +151,8 @@
     groups = len(lists[0])
     streams = [[piece for group in groups_s for piece in group[-1]] for groups_s in lists]
     pairs = len(streams[0])
+    head = [stream[0] for stream in streams]
+    last = [stream[-1] for stream in streams]
     early = [piece[0] for pair in zip(*streams) for piece in pair]
     grads, weights, moments = take(6), take(6), take(6)
     norm_inputs = take(3)
@@ -163,7 +163,7 @@
     send_3, recv_3, keep_3 = (take(2 * groups) for _ in range(3))
     norm_held = take(3)
     norm_send, norm_recv, norm_full = take(3)
-    sems, send_sems, group_sems, norm_sems = take(4)
+    sems, send_sems, group_sems, norm_sems, cross_sems = take(5)
 
     me = lax.axis_index("batch")
     c = lax.rem(me, 2)
@@ -212,15 +212,23 @@
         first = other_x if x_first else other_y
         at = pl.ds(row, rows)
         place = gathered[m]
+        full = place.at[:, :, c, at, :]
         half = place.at[:, x, c, at, :] if x_first else place.at[y, :, c, at, :]
         source, target, device = (
-            (send_1[i], recv_1[i], other_c),
-            (send_2[i], recv_2[i], first),
+            (send_1[i], recv_1[i], first if piece in head else other_c),
+            (send_2[i], recv_2[i], other_c if piece in head else first),
             (half, half, first),
-            (place.at[:, :, c, at, :], place.at[:, :, c, at, :], other_c),
+            (half, half, other_c) if piece in last else (full, full, other_c),
         )[step]
         kind = (CORE, FIRST, LOAD, CORE)[step]
         return remote(source, target, send_sems.at[m], sems.at[i, kind], device)
+
+    def cross_hop(piece):
+        i, m, row, rows, x_first = piece
+        at = pl.ds(row, rows)
+        half = gathered[m].at[:, x, c, at, :] if x_first else gathered[m].at[y, :, c, at, :]
+        device = (other_x if x_first else other_y) + 1 - 2 * c
+        return remote(half, half, send_sems.at[m], cross_sems.at[0 if x_first else 1], device)
 
     def group_hop(group, step):
         g, m, row, rows, x_first, _ = group
@@ -245,24 +253,39 @@
     def spot(x_first, first, second):
         return 2 * second + first if x_first else 2 * first + second
 
+    def shares(piece):
+        f = x if piece[-1] else y
+
+        def owner(first, second, core):
+            return 2 * spot(piece[-1], first, second) + core
+
+        if piece in head:
+            return (
+                [owner(1 - f, q // 2, q % 2) for q in range(4)],
+                [(owner(f, second, 1 - c), 2 * second + 1 - c) for second in range(2)],
+                [(owner(f, second, c), 2 * second + c) for second in range(2)],
+            )
+        return (
+            [2 * q + 1 - c for q in range(4)],
+            [(owner(1 - f, second, c), spot(piece[-1], 1 - f, second)) for second in range(2)],
+            [(owner(f, second, c), spot(piece[-1], f, second)) for second in range(2)],
+        )
+
     def give(piece):
+        load(piece).wait()
+        for q, owner in enumerate(shares(piece)[0]):
+            send_1[piece[0]][q] = block(piece, owner).astype(jnp.bfloat16)
+
+    def add_core(piece):
         i = piece[0]
-        load(piece).wait()
-        for q in range(4):
-            send_1[i][q] = block(piece, 2 * q + 1 - c).astype(jnp.bfloat16)
-
-    def add_core(piece):
-        i, x_first = piece[0], piece[-1]
-        f = x if x_first else y
+        _, given, kept = shares(piece)
         hop(piece, 0).wait_recv()
-        for second in range(2):
-            q = spot(x_first, 1 - f, second)
-            total = block(piece, 2 * q + c) + recv_1[i][q].astype(jnp.float32)
-            send_2[i][second] = total.astype(jnp.bfloat16)
+        for j, (owner, q) in enumerate(given):
+            total = block(piece, owner) + recv_1[i][q].astype(jnp.float32)
+            send_2[i][j] = total.astype(jnp.bfloat16)
         hop(piece, 1).start()
-        for second in range(2):
-            q = spot(x_first, f, second)
-            keep_2[i][second] = block(piece, 2 * q + c) + recv_1[i][q].astype(jnp.float32)
+        for j, (owner, q) in enumerate(kept):
+            keep_2[i][j] = block(piece, owner) + recv_1[i][q].astype(jnp.float32)
 
     def add_first(group):
         g, m, start, _, x_first, pieces = group
@@ -292,12 +315,19 @@
         group_hop(group, 1).wait_recv()
         for piece in group[-1]:
             hop(piece, 2).start()
+            if piece in last:
+                cross_hop(piece).start()
+                hop(piece, 3).start()
 
     def pass_on(piece):
-        hop(piece, 2).wait_recv()
-        hop(piece, 3).start()
+        if piece not in last:
+            hop(piece, 2).wait_recv()
+            hop(piece, 3).start()
 
     def finish(piece):
+        if piece in last:
+            hop(piece, 2).wait_recv()
+            cross_hop(piece).wait_recv()
         hop(piece, 3).wait_recv()
 
     def norm_loads():
@@ -364,7 +394,10 @@
         if p == pairs - 1:
             for copy in norm_loads():
                 copy.start()
-        both(add_core, in_pairs[p - 1])
+        if p > 1:
+            both(add_core, in_pairs[p - 1])
+        if p == LATE:
+            both(add_core, in_pairs[0])
     both(params_wait, range(6))
     norm_stage(0)
     for i, pair in enumerate(group_pairs):
@@ -467,6 +500,7 @@
             pltpu.SemaphoreType.DMA((6,)),
             pltpu.SemaphoreType.DMA((len(groups), 2)),
             pltpu.SemaphoreType.DMA((4,)),
+            pltpu.SemaphoreType.DMA((2,)),
         ],
         compiler_params=pltpu.CompilerParams(
             collective_id=0, has_side_effects=True, vmem_limit_bytes=40 * 2**20

time: 63.6 us -> 63.1 us (level)
  no operation moved by 1% of the time
where the time goes in v3:
time: 63.1 us; the launch traced here: 62.9 us
  Pallas kernels  62.2 us (99%)
  between operations  0.67 us (1%)
    pallas_call x1, Pallas kernels, kernel_body(): pl.pallas_call(functools.partial(exchange, shapes, n), out_shape=parts +...  58.5 us
    pallas_call x1, Pallas kernels, kernel_body(): pl.pallas_call(functools.partial(write_out, shapes, n), out_shape=[part i...  3.74 us

profile of v3, /device:TPU:0, one launch (start us, length us, event | category | flops | bytes accessed | tf_op | source)
XLA Modules:
  0.0 62.9 jit_solution(9443390366425661607)
XLA Ops:
  0.7 58.5 %shard_map.364 = (bf16[2,2,2,128,1024]{4,3,2,1,0:T(8,128)(2,1)S(1)}, bf16[2,2,2,1024,128]{4,3,2,1,0:T(8,128)(2,1)S(1)}, bf16[2,2,2,128,256]{4,3,2,1,0:T(8,128)(2...) custom-call(f32[8,128,1024]{2,1,0:T(8,128)} %bitcast.15, ...), custom_call_target="tpu_custom_call" | custom-call | tf_op jit(solution)/shard_map/pallas_call | solution.py:482
  59.2 3.7 %shard_map.365 = (bf16[2,2,2,128,1024]{4,3,2,1,0:T(8,128)(2,1)}, bf16[1024,1024]{1,0:T(8,128)(2,1)}, bf16[2,2,2,128,256]{4,3,2,1,0:T(8,128)(2,1)}, bf16[2,2,2,12...) custom-call(bf16[2,2,2,128,1024]{4,3,2,1,0:T(8,128)(2,1)S(1)} %get-t, ...), custom_call_target="tpu_custom_call" | custom-call | tf_op jit(solution)/shard_map/pallas_call | solution.py:509

commit v4 on v3

--- a/solution.py
+++ b/solution.py
@@ -117,7 +117,7 @@
 
 PLANS = (((2, ((1, 3),)), (0, ((1, 1), (2,))), (3, ((3, 1),))), ((4, ((1, 3),)), (1, ((1, 1), (2,))), (5, ((3, 1),))))
 LEAD = 2
-LATE = 4
+LATE = 3
 BY_ROWS = (True, False, True, True, True, False)
 LOAD, CORE, FIRST, KINDS = 0, 1, 2, 3
 
@@ -231,11 +231,12 @@
         return remote(half, half, send_sems.at[m], cross_sems.at[0 if x_first else 1], device)
 
     def group_hop(group, step):
-        g, m, row, rows, x_first, _ = group
+        g, m, row, rows, x_first, pieces = group
         second = other_y if x_first else other_x
         place = gathered[m].at[y, x, c, pl.ds(row, rows), :]
         source, target = ((send_3[g], recv_3[g]), (place, place))[step]
-        return remote(source, target, send_sems.at[m], group_sems.at[g, step], second)
+        recv_sem = (group_sems.at[g], sems.at[pieces[0][0], FIRST])[step]
+        return remote(source, target, send_sems.at[m], recv_sem, second)
 
     def sent(m):
         width = shapes[m][1]
@@ -498,7 +499,7 @@
         + [
             pltpu.SemaphoreType.DMA((len(pieces), KINDS)),
             pltpu.SemaphoreType.DMA((6,)),
-            pltpu.SemaphoreType.DMA((len(groups), 2)),
+            pltpu.SemaphoreType.DMA((len(groups),)),
             pltpu.SemaphoreType.DMA((4,)),
             pltpu.SemaphoreType.DMA((2,)),
         ],

time: 63.1 us -> 63 us (level)
  no operation moved by 1% of the time
where the time goes in v4:
time: 63 us; the launch traced here: 62.8 us
  Pallas kernels  62.2 us (99%)
  between operations  0.67 us (1%)
    pallas_call x1, Pallas kernels, kernel_body(): pl.pallas_call(functools.partial(exchange, shapes, n), out_shape=parts +...  58.4 us
    pallas_call x1, Pallas kernels, kernel_body(): pl.pallas_call(functools.partial(write_out, shapes, n), out_shape=[part i...  3.74 us

profile of v4, /device:TPU:0, one launch (start us, length us, event | category | flops | bytes accessed | tf_op | source)
XLA Modules:
  0.0 62.8 jit_solution(15711907255544408588)
XLA Ops:
  0.7 58.4 %shard_map.364 = (bf16[2,2,2,128,1024]{4,3,2,1,0:T(8,128)(2,1)S(1)}, bf16[2,2,2,1024,128]{4,3,2,1,0:T(8,128)(2,1)S(1)}, bf16[2,2,2,128,256]{4,3,2,1,0:T(8,128)(2...) custom-call(f32[8,128,1024]{2,1,0:T(8,128)} %bitcast.15, ...), custom_call_target="tpu_custom_call" | custom-call | tf_op jit(solution)/shard_map/pallas_call | solution.py:483
  59.1 3.7 %shard_map.365 = (bf16[2,2,2,128,1024]{4,3,2,1,0:T(8,128)(2,1)}, bf16[1024,1024]{1,0:T(8,128)(2,1)}, bf16[2,2,2,128,256]{4,3,2,1,0:T(8,128)(2,1)}, bf16[2,2,2,12...) custom-call(bf16[2,2,2,128,1024]{4,3,2,1,0:T(8,128)(2,1)S(1)} %get-t, ...), custom_call_target="tpu_custom_call" | custom-call | tf_op jit(solution)/shard_map/pallas_call | solution.py:510
